TPU v7x, 32 devices: a whole 2x2x4 slice. The times are simulated.
32 devices in a mesh: rep: 1, r: 8 (over y, z), s: 4 (over x, core).
Axes of the slice: x: 2, y: 2, z: 4, core: 2. Of those that a mesh axis runs over, the one named last changes fastest.
Arguments:
- x: bfloat16 [32, 4096, 768], P(('rep', 'r', 's'))
- dy: bfloat16 [32, 4096, 768], P(('rep', 'r', 's'))
- w_gate: bfloat16 [2, 768, 1792], P(None, 's')
- w_up: bfloat16 [2, 768, 1792], P(None, 's')
- w_down: bfloat16 [2, 1792, 768], P(None, 's')
Outputs:
- output 1: bfloat16 [32, 4096, 768], P(('rep', 'r', 's'))
- output 2: bfloat16 [2, 768, 1792], P('rep', 's')
- output 3: bfloat16 [2, 768, 1792], P('rep', 's')
- output 4: bfloat16 [2, 1792, 768], P('rep', 's')
All inputs are finite; a program needn't handle non-finite values.
Results may differ from a plain program's by a relative error of at most 0.018.
Values are sent between devices in bfloat16 or wider.
A program may use at most 2 GiB of HBM per device.

v0:
```python
import jax
import jax.numpy as jnp
from jax import lax
from jax.sharding import PartitionSpec as P

NAMES = ("w_gate", "w_up", "w_down")


def matmul(a, w):
    return jnp.dot(a, w, preferred_element_type=jnp.float32).astype(jnp.bfloat16)


def normed(h):
    wide = h.astype(jnp.float32)
    scale = lax.rsqrt(jnp.mean(wide**2, -1, keepdims=True) + 1e-6)
    return (wide * scale).astype(jnp.bfloat16)


def layer(h, w):
    a = normed(h)
    gate = jnp.dot(a, w["w_gate"], preferred_element_type=jnp.float32)
    up = jnp.dot(a, w["w_up"], preferred_element_type=jnp.float32)
    return h + matmul((jax.nn.silu(gate) * up).astype(jnp.bfloat16), w["w_down"])


def solution(mesh):
    def fetched(weights, number):
        return {name: lax.all_gather(w[number], "s", axis=0, tiled=True) for name, w in zip(NAMES, weights, strict=True)}

    def summed(term):
        return lax.psum(lax.psum_scatter(term, "s", scatter_dimension=0, tiled=True), "r")

    def step(x, dy, *weights):
        layers = weights[0].shape[0]
        h, inputs = x[0], []
        for number in range(layers):
            inputs.append(h)
            h = layer(h, fetched(weights, number))
        by_h, mine = dy[0], [None] * layers
        for number in reversed(range(layers)):
            _, back = jax.vjp(lambda w, h: layer(h, w), fetched(weights, number), inputs[number])
            by_w, by_h = back(by_h)
            mine[number] = [summed(by_w[name]) for name in NAMES]
        return (by_h[None], *(jnp.stack([mine[number][i] for number in range(layers)]) for i in range(3)))

    states, cut = P(("rep", "r", "s"), None, None), P(None, "s", None)
    return jax.shard_map(
        step,
        mesh=mesh,
        in_specs=(states, states) + (cut,) * 3,
        out_specs=(states,) + (P("rep", "s", None),) * 3,
        check_vma=False,
    )
```

profile of v0, /device:TPU:0, one launch (start us, length us, event | category | flops | bytes accessed | tf_op | source)
XLA Modules:
  0.0 697.6 jit_solution(7954877673128067783)
XLA Ops:
  29.9 8.7 %copy.9 = bf16[1,4096,768]{1,2,0:T(8,128)(2,1)} copy(bf16[1,4096,768]{2,1,0:T(8,128)(2,1)} %param.6) | data formatting | bytes 12582912 | tf_op args[1]
  38.9 19.8 %fusion.42 = f32[4096,1792]{1,0:T(8,128)} fusion(bf16[1,4096,768]{1,2,0:T(8,128)(2,1)} %copy.10, f32[4096]{0:T(1024)S(1)} %fusion.70, bf16[1,768,1792]{2,1,0:T(8,128)(2,1)} %all-gather.13.cloned.1.call-done), kind=kOutput, calls=%fused_computation.61 | convolution fusion | flops 11283726336 | bytes 38420480 | tf_op jit(solution)/shard_map/dot_general | solution.py:21
  66.4 33.6 %multiply_convert_fusion.1 = (bf16[4096,1792]{1,0:T(8,128)(2,1)}, f32[4096,1792]{1,0:T(8,128)}) fusion(f32[4096,1792]{1,0:T(8,128)} %fusion.42, bf16[1,768,1792]{2,1,0:T(8,128)(2,1)} %all-gather.15.cloned.1.call-done, bf16[1,4096,768]{1,2,0:T(8,128)(2,1)} %copy.10, f32[4096]{0:T(1024)S(1)} %fusion.70), kind=kOutput, calls=%fused_computation.13 | convolution fusion | flops 11327766528 | bytes 82460672 | tf_op jit(solution)/shard_map/dot_general | solution.py:22
  100.0 19.4 %fusion.18 = (f32[4096]{0:T(1024)S(1)}, bf16[4096,768]{0,1:T(8,128)(2,1)}) fusion(bf16[4096,1792]{1,0:T(8,128)(2,1)} %get-tuple-element.20, bf16[1,1792,768]{2,1,0:T(8,128)(2,1)} %all-gather.17.cloned.1.call-done, bf16[1,4096,768]{1,2,0:T(8,128)(2,1)} %copy.10), kind=kOutput, calls=%fused_computation.40 | convolution fusion | flops 11290013696 | bytes 30031872 | tf_op jit(solution)/shard_map/dot_general | solution.py:10
  122.0 19.9 %fusion.33 = f32[4096,1792]{1,0:T(8,128)} fusion(bf16[4096,768]{0,1:T(8,128)(2,1)} %get-tuple-element.23, f32[4096]{0:T(1024)S(1)} %fusion.71, bf16[1,768,1792]{2,1,0:T(8,128)(2,1)} %all-gather.23.cloned.1.call-done), kind=kOutput, calls=%fused_computation.57 | convolution fusion | flops 11283726336 | bytes 38420480 | tf_op jit(solution)/shard_map/jvp()/dot_general | solution.py:22
  149.4 17.5 %convolution_convert_fusion.1 = bf16[4096,1792]{1,0:T(8,128)(2,1)} fusion(bf16[1,4096,768]{2,1,0:T(8,128)(2,1)} %param.6, bf16[1,1792,768]{2,1,0:T(8,128)(2,1)} %all-gather.21.cloned.1.call-done), kind=kOutput, calls=%fused_computation.31 | convolution fusion | flops 11281629184 | bytes 23724032 | tf_op jit(solution)/shard_map/transpose(jvp())/dot_general | solution.py:10
  166.9 10.4 %all-gather.19.cloned.1.call-done = bf16[1,768,1792]{2,1,0:T(8,128)(2,1)} async-done(((bf16[1,192,1792]{2,1,0:T(8,128)(2,1)}), bf16[1,768,1792]{2,1,0:T(8,128)(2,1)}) %all-gather.19.cloned.1.call-update) | async-done | bytes 2752528 | tf_op jit(solution)/shard_map/all_gather | solution.py:28
  177.3 39.8 %fusion.1 = (bf16[4096,1792]{1,0:T(8,128)(2,1)}, f32[4096,1792]{1,0:T(8,128)}) fusion(f32[4096,1792]{1,0:T(8,128)} %fusion.33, bf16[4096,1792]{1,0:T(8,128)(2,1)} %convolution_convert_fusion.1, bf16[1,768,1792]{2,1,0:T(8,128)(2,1)} %all-gather.19.cloned.1.call-done, bf16[4096,768]{0,1:T(8,128)(2,1)} %get-tuple-element.23, f32[4096]{0:T(1024)S(1)} %fusion.71), kind=kOutput, calls=%fused_computation.7 | convolution fusion | flops 11371806720 | bytes 97140736 | tf_op jit(solution)/shard_map/jvp()/dot_general | solution.py:21
  217.2 22.1 %fusion.22 = bf16[4096,768]{0,1:T(8,128)(2,1)} fusion(bf16[4096,1792]{1,0:T(8,128)(2,1)} %convolution_convert_fusion.1, bf16[1,768,1792]{2,1,0:T(8,128)(2,1)S(1)} %copy-done.11, f32[4096,1792]{1,0:T(8,128)} %get-tuple-element.25), kind=kOutput, calls=%fused_computation.44 | convolution fusion | flops 11321475072 | bytes 53084160 | tf_op jit(solution)/shard_map/transpose(jvp())/dot_general | solution.py:22
  239.3 21.1 %fusion.20 = (f32[4096]{0:T(1024)S(1)}, bf16[4096,768]{0,1:T(8,128)(2,1)}) fusion(bf16[4096,768]{0,1:T(8,128)(2,1)} %get-tuple-element.23, bf16[4096,768]{0,1:T(8,128)(2,1)} %fusion.22, bf16[4096,1792]{1,0:T(8,128)(2,1)} %get-tuple-element.24, bf16[1,768,1792]{2,1,0:T(8,128)(2,1)} %all-gather.19.cloned.1.call-done), kind=kOutput, calls=%fused_computation.42 | convolution fusion | flops 11290013696 | bytes 36323328 | tf_op jit(solution)/shard_map/transpose(jvp())/dot_general | solution.py:21
  260.4 9.5 %fusion.25 = bf16[4096,768]{0,1:T(8,128)(2,1)} fusion(bf16[4096,768]{0,1:T(8,128)(2,1)} %get-tuple-element.23, bf16[4096,768]{0,1:T(8,128)(2,1)} %get-tuple-element.27, bf16[1,4096,768]{1,2,0:T(8,128)(2,1)S(1)} %copy-done, f32[4096]{0:T(1024)S(1)} %multiply_multiply_fusion.1, f32[4096]{0:T(1024)S(1)} %fusion.71), kind=kLoop, calls=%fused_computation.50 | loop fusion | flops 22020096 | bytes 25198592 | tf_op jit(solution)/shard_map/transpose(jvp())/add_any | solution.py:14
  269.9 17.8 %convolution_convert_fusion.5 = bf16[1792,768]{1,0:T(8,128)(2,1)} fusion(bf16[4096,1792]{1,0:T(8,128)(2,1)} %get-tuple-element.20, bf16[4096,768]{0,1:T(8,128)(2,1)} %fusion.25), kind=kOutput, calls=%fused_computation.62 | convolution fusion | flops 11275665408 | bytes 23724032 | tf_op jit(solution)/shard_map/transpose(jvp())/dot_general | solution.py:10
  287.8 26.2 %fusion.50 = bf16[1792,768]{1,0:T(8,128)(2,1)} fusion(bf16[1,4096,768]{2,1,0:T(8,128)(2,1)} %param.6, f32[4096,1792]{1,0:T(8,128)} %fusion.33, f32[4096,1792]{1,0:T(8,128)} %get-tuple-element.25), kind=kOutput, calls=%fused_computation.65 | convolution fusion | flops 11319705600 | bytes 67764224 | tf_op jit(solution)/shard_map/transpose(jvp())/dot_general | solution.py:10
  314.1 39.7 %fusion.3 = (bf16[4096,1792]{1,0:T(8,128)(2,1)}, bf16[4096,1792]{1,0:T(8,128)(2,1)}) fusion(f32[4096,1792]{1,0:T(8,128)} %fusion.42, f32[4096,1792]{1,0:T(8,128)} %get-tuple-element.21, bf16[4096,768]{0,1:T(8,128)(2,1)} %fusion.25, bf16[1,1792,768]{2,1,0:T(8,128)(2,1)S(1)} %copy-done.10), kind=kOutput, calls=%fused_computation.9 | convolution fusion | flops 11369709568 | bytes 97124352 | tf_op jit(solution)/shard_map/transpose(jvp())/dot_general | solution.py:10
  353.8 25.2 %fusion.53 = bf16[768,1792]{1,0:T(8,128)(2,1)} fusion(bf16[4096,1792]{1,0:T(8,128)(2,1)} %get-tuple-element.29, bf16[1,4096,768]{1,2,0:T(8,128)(2,1)} %copy.10, f32[4096]{0:T(1024)S(1)} %copy-done.4, f32[4096,1792]{1,0:T(8,128)} %fusion.42), kind=kOutput, calls=%fused_computation.66 | convolution fusion | flops 11329142784 | bytes 53100544 | tf_op jit(solution)/shard_map/transpose(jvp())/dot_general | solution.py:22
  379.1 25.2 %fusion.56 = bf16[768,1792]{1,0:T(8,128)(2,1)} fusion(bf16[4096,1792]{1,0:T(8,128)(2,1)} %convolution_convert_fusion.1, bf16[4096,768]{0,1:T(8,128)(2,1)} %get-tuple-element.23, f32[4096]{0:T(1024)S(1)} %copy-done.6, f32[4096,1792]{1,0:T(8,128)} %get-tuple-element.25), kind=kOutput, calls=%fused_computation.67 | convolution fusion | flops 11329142784 | bytes 53100544 | tf_op jit(solution)/shard_map/transpose(jvp())/dot_general | solution.py:22
  404.4 18.6 %fusion.47 = bf16[768,1792]{1,0:T(8,128)(2,1)} fusion(bf16[4096,1792]{1,0:T(8,128)(2,1)} %get-tuple-element.24, bf16[4096,768]{0,1:T(8,128)(2,1)} %get-tuple-element.23, f32[4096]{0:T(1024)S(1)} %copy-done.6), kind=kOutput, calls=%fused_computation.64 | convolution fusion | flops 11283726336 | bytes 23740416 | tf_op jit(solution)/shard_map/transpose(jvp())/dot_general | solution.py:21
  423.1 18.6 %fusion.44 = bf16[768,1792]{1,0:T(8,128)(2,1)} fusion(bf16[4096,1792]{1,0:T(8,128)(2,1)} %get-tuple-element.28, bf16[1,4096,768]{1,2,0:T(8,128)(2,1)} %copy.10, f32[4096]{0:T(1024)S(1)} %copy-done.4), kind=kOutput, calls=%fused_computation.63 | convolution fusion | flops 11283726336 | bytes 23740416 | tf_op jit(solution)/shard_map/transpose(jvp())/dot_general | solution.py:21
  441.8 23.3 %fusion.21 = bf16[4096,768]{0,1:T(8,128)(2,1)} fusion(bf16[4096,1792]{1,0:T(8,128)(2,1)} %get-tuple-element.29, bf16[1,768,1792]{2,1,0:T(8,128)(2,1)} %all-gather.15.cloned.1.call-done, f32[4096,1792]{1,0:T(8,128)} %fusion.42), kind=kOutput, calls=%fused_computation.43 | convolution fusion | flops 11321475072 | bytes 53084160 | tf_op jit(solution)/shard_map/transpose(jvp())/dot_general | solution.py:22
  465.2 24.2 %reduce-scatter.9.cloned.1.call-done = bf16[192,1792]{1,0:T(8,128)(2,1)} async-done(((bf16[768,1792]{1,0:T(8,128)(2,1)}), bf16[192,1792]{1,0:T(8,128)(2,1)}) %reduce-scatter.9.cloned.1.call-update) | async-done | bytes 688144 | tf_op jit(solution)/shard_map/reduce_scatter | solution.py:31
  489.4 37.5 %reduce-scatter.7.cloned.1.call-done = bf16[192,1792]{1,0:T(8,128)(2,1)} async-done(((bf16[768,1792]{1,0:T(8,128)(2,1)}), bf16[192,1792]{1,0:T(8,128)(2,1)}) %reduce-scatter.7.cloned.1.call-update) | async-done | bytes 688144 | tf_op jit(solution)/shard_map/reduce_scatter | solution.py:31
  527.0 26.0 %fusion.17 = (f32[4096]{0:T(1024)S(1)}, bf16[4096,768]{0,1:T(8,128)(2,1)S(1)}) fusion(bf16[1,4096,768]{1,2,0:T(8,128)(2,1)} %copy.10, bf16[4096,768]{0,1:T(8,128)(2,1)} %fusion.21, bf16[4096,1792]{1,0:T(8,128)(2,1)} %get-tuple-element.28, bf16[1,768,1792]{2,1,0:T(8,128)(2,1)S(1)} %copy-done.9), kind=kOutput, calls=%fused_computation.39 | convolution fusion | flops 11290013696 | bytes 36323328 | tf_op jit(solution)/shard_map/transpose(jvp())/dot_general | solution.py:21
  553.0 9.5 %fusion.24 = bf16[1,4096,768]{1,2,0:T(8,128)(2,1)} fusion(bf16[4096,768]{0,1:T(8,128)(2,1)} %fusion.25, bf16[4096,768]{0,1:T(8,128)(2,1)S(1)} %get-tuple-element.31, bf16[1,4096,768]{1,2,0:T(8,128)(2,1)} %copy.10, f32[4096]{0:T(1024)S(1)} %multiply_multiply_fusion, f32[4096]{0:T(1024)S(1)} %copy-done.4), kind=kLoop, calls=%fused_computation.49 | loop fusion | flops 22020096 | bytes 25198592 | tf_op jit(solution)/shard_map/broadcast_in_dim | solution.py:44
  571.1 113.5 %all-reduce.3.cloned.1.call-done = (bf16[1,192,1792]{2,1,0:T(8,128)(2,1)}, bf16[1,192,1792]{2,1,0:T(8,128)(2,1)}, bf16[1,192,1792]{2,1,0:T(8,128)(2,1)}, bf16[1,...) async-done(((bf16[1,192,1792]{2,1,0:T(8,128)(2,1)}, bf16[1,192,1792]{2,1,0:T(8,128)(2,1)}, bf16[1,192,1792]{2,1,0:T(8,128)(2,1)}, ...) | async-done | bytes 4128784 | tf_op jit(solution)/shard_map/psum | solution.py:31
  (71 shorter events, 55.8 us)
Async XLA Ops:
  7.2 31.7 %all-gather.13.cloned.1.call-start = ((), (), s32[]{:S(2)}) async-start(), calls=%async_computation.12 | async-start | bytes 3440640 | tf_op jit(solution)/shard_map/all_gather | solution.py:28
  9.7 56.7 %all-gather.15.cloned.1.call-start = ((), (), s32[]{:S(2)}) async-start(), calls=%async_computation.13 | async-start | bytes 3440640 | tf_op jit(solution)/shard_map/all_gather | solution.py:28
  12.3 87.7 %all-gather.17.cloned.1.call-start = ((), (), s32[]{:S(2)}) async-start(), calls=%async_computation.14 | async-start | bytes 3440640 | tf_op jit(solution)/shard_map/all_gather | solution.py:28
  14.8 107.1 %all-gather.23.cloned.1.call-start = ((), (), s32[]{:S(2)}) async-start(), calls=%async_computation.17 | async-start | bytes 3440640 | tf_op jit(solution)/shard_map/all_gather | solution.py:28
  15.4 133.9 %all-gather.21.cloned.1.call-start = ((), (), s32[]{:S(2)}) async-start(), calls=%async_computation.16 | async-start | bytes 3440640 | tf_op jit(solution)/shard_map/all_gather | solution.py:28
  16.0 161.3 %all-gather.19.cloned.1.call-start = ((), (), s32[]{:S(2)}) async-start(), calls=%async_computation.15 | async-start | bytes 3440640 | tf_op jit(solution)/shard_map/all_gather | solution.py:28
  16.6 448.6 %reduce-scatter.15.cloned.1.call-start = ((), (), s32[]{:S(2)}) async-start(), calls=%async_computation.10 | async-start | bytes 3440640 | tf_op jit(solution)/shard_map/reduce_scatter | solution.py:31
  29.9 36.5 %copy-start.3 = (f32[4096]{0:T(1024)}, f32[4096]{0:T(1024)S(1)}, u32[]{:S(2)}) copy-start(f32[4096]{0:T(1024)S(1)} %fusion.70) | copy-start | bytes 49156
  119.4 22.5 %copy-start.7 = (f32[4096]{0:T(1024)}, f32[4096]{0:T(1024)S(1)}, u32[]{:S(2)}) copy-start(f32[4096]{0:T(1024)S(1)} %get-tuple-element.22) | copy-start | bytes 49156
  119.4 141.0 %copy-start.5 = (f32[4096]{0:T(1024)}, f32[4096]{0:T(1024)S(1)}, u32[]{:S(2)}) copy-start(f32[4096]{0:T(1024)S(1)} %fusion.71) | copy-start | bytes 49156
  166.9 50.3 %copy-start.11 = (bf16[1,768,1792]{2,1,0:T(8,128)(2,1)S(1)}, bf16[1,768,1792]{2,1,0:T(8,128)(2,1)}, u32[]{:S(2)}) copy-start(bf16[1,768,1792]{2,1,0:T(8,128)(2,1)} %all-gather.23.cloned.1.call-done) | copy-start | bytes 8257540
  239.3 21.1 %copy-start.8 = (f32[4096]{0:T(1024)S(1)}, f32[4096]{0:T(1024)}, u32[]{:S(2)}) copy-start(f32[4096]{0:T(1024)} %copy-done.7) | copy-start | bytes 49156
  239.3 21.2 %copy-start = (bf16[1,4096,768]{1,2,0:T(8,128)(2,1)S(1)}, bf16[1,4096,768]{1,2,0:T(8,128)(2,1)}, u32[]{:S(2)}) copy-start(bf16[1,4096,768]{1,2,0:T(8,128)(2,1)} %copy.9) | copy-start | bytes 18874372
  287.7 26.4 %copy-start.10 = (bf16[1,1792,768]{2,1,0:T(8,128)(2,1)S(1)}, bf16[1,1792,768]{2,1,0:T(8,128)(2,1)}, u32[]{:S(2)}) copy-start(bf16[1,1792,768]{2,1,0:T(8,128)(2,1)} %all-gather.17.cloned.1.call-done) | copy-start | bytes 8257540
  287.7 177.4 %reduce-scatter.17.cloned.1.call-start = ((), (), s32[]{:S(2)}) async-start(), calls=%async_computation.11 | async-start | bytes 3440640 | tf_op jit(solution)/shard_map/reduce_scatter | solution.py:31
  314.0 151.2 %reduce-scatter.11.cloned.1.call-start = ((), (), s32[]{:S(2)}) async-start(), calls=%async_computation.8 | async-start | bytes 3440640 | tf_op jit(solution)/shard_map/reduce_scatter | solution.py:31
  314.1 39.7 %copy-start.4 = (f32[4096]{0:T(1024)S(1)}, f32[4096]{0:T(1024)}, u32[]{:S(2)}) copy-start(f32[4096]{0:T(1024)} %copy-done.3) | copy-start | bytes 49156
  353.8 25.3 %copy-start.6 = (f32[4096]{0:T(1024)S(1)}, f32[4096]{0:T(1024)}, u32[]{:S(2)}) copy-start(f32[4096]{0:T(1024)} %copy-done.5) | copy-start | bytes 49156
  379.0 86.2 %reduce-scatter.13.cloned.1.call-start = ((), (), s32[]{:S(2)}) async-start(), calls=%async_computation.9 | async-start | bytes 3440640 | tf_op jit(solution)/shard_map/reduce_scatter | solution.py:31
  404.3 85.1 %reduce-scatter.9.cloned.1.call-start = ((), (), s32[]{:S(2)}) async-start(), calls=%async_computation.7 | async-start | bytes 3440640 | tf_op jit(solution)/shard_map/reduce_scatter | solution.py:31
  423.0 103.9 %reduce-scatter.7.cloned.1.call-start = ((), (), s32[]{:S(2)}) async-start(), calls=%async_computation.6 | async-start | bytes 3440640 | tf_op jit(solution)/shard_map/reduce_scatter | solution.py:31
  441.8 85.2 %copy-start.9 = (bf16[1,768,1792]{2,1,0:T(8,128)(2,1)S(1)}, bf16[1,768,1792]{2,1,0:T(8,128)(2,1)}, u32[]{:S(2)}) copy-start(bf16[1,768,1792]{2,1,0:T(8,128)(2,1)} %all-gather.13.cloned.1.call-done) | copy-start | bytes 8257540
  441.8 242.8 %all-reduce.3.cloned.1.call-start = ((), (), s32[]{:S(2)}) async-start(), calls=%async_computation.18 | async-start | bytes 8257536 | tf_op jit(solution)/shard_map/psum | solution.py:31
  527.0 26.0 %copy-start.2 = (f32[4096]{0:T(1024)S(1)}, f32[4096]{0:T(1024)}, u32[]{:S(2)}) copy-start(f32[4096]{0:T(1024)} %copy-done.1) | copy-start | bytes 49156
  (1 other events, 0.6 us)
Sparse Core Ops, SparseCore 0:
  10.1 28.7 all-gather.12
  40.4 25.9 all-gather.14
  68.0 25.9 all-gather.16
  96.0 25.9 all-gather.22
  123.4 25.9 all-gather.20
  151.3 25.9 all-gather.18
  287.8 35.0 reduce-scatter.14
  325.5 35.0 reduce-scatter.16
  379.1 35.0 reduce-scatter.10
  416.6 35.0 reduce-scatter.12
  454.3 35.0 reduce-scatter.8
  491.8 35.0 reduce-scatter.6
  531.3 153.3 all-reduce.2
where the time goes:
time: 705 us; the launch traced here: 698 us
  matrix products  414 us (59%)
  waiting for transfers between devices  205 us (29%)
  local copies, waits for them, and re-layouts  34 us (5%)
  other arithmetic  29.1 us (4%)
  between operations  14.5 us (2%)
    dot_general x6, matrix products, layer(): up = jnp.dot(a, w['w_up'], preferred_element_type=jnp.float32)  149 us
    dot_general x6, matrix products, layer(): gate = jnp.dot(a, w['w_gate'], preferred_element_type=jnp.float32)  144 us
    dot_general x5, matrix products, matmul(): jnp.dot(a, w, preferred_element_type=jnp.float32).astype(jnp.bfloat16)  121 us
    psum x1, waiting for transfers between devices, summed(): lax.psum(lax.psum_scatter(term, 's', scatter_dimension=0, tiled=True), 'r')  113 us
    reduce_scatter x6, waiting for transfers between devices, summed(): lax.psum_scatter(term, 's', scatter_dimension=0, tiled=True)  61.8 us
    all_gather x6, waiting for transfers between devices, fetched(): lax.all_gather(w[number], 's', axis=0, tiled=True)  28.4 us
    unnamed x27, local copies, waits for them, and re-layouts  26.6 us
  transfers between devices with their start and end apart: 13, of which 8 were waited for; matrix products, arithmetic and copies ran while one was open for 51% of the time, Pallas kernels for 0%

commit v1 on v0

v1 whole, which is shorter than its diff:
```python
import functools
import jax
import jax.numpy as jnp
from jax import lax
from jax.experimental import pallas as pl
from jax.experimental.pallas import tpu as pltpu
from jax.sharding import PartitionSpec as P

F32, BF = jnp.float32, jnp.bfloat16
MESH = pl.DeviceIdType.MESH
TOK, D, FF = 4096, 768, 1792
T = TOK // 8
ANY = pl.BlockSpec(memory_space=pl.ANY)


def dot(a, b):
    return jnp.dot(a, b, preferred_element_type=F32)


def dot_nt(a, b):
    return lax.dot_general(a, b, (((1,), (1,)), ((), ())), preferred_element_type=F32)


def dot_tn(a, b):
    return lax.dot_general(a, b, (((0,), (0,)), ((), ())), preferred_element_type=F32)


def sigmoid(g):
    return 0.5 + 0.5 * jnp.tanh(0.5 * g)


def place():
    r, s = lax.axis_index("r"), lax.axis_index("s")
    return r, r // 4, lax.rem(r, 4), s, s // 2, lax.rem(s, 2)


def forward_kernel(x_hbm, wg_in, wu_in, wd_in,
                   h1_hbm, gate_hbm, up_hbm, at_hbm, w0g, w0u, w0d, w1g, w1u, w1d,
                   wg_v, wu_v, wd_v, og, ou, od, a_v, gate_v, hin, up_s, at_s, hid_s, h1_s,
                   sa_s, sa_r, sr_s, sr_r, sp_s, sp_r, so_s, so_r, s_loc, s_hin, s_up, s_at, s_h1, s_gate, s_w0):
    r, y, z, s, x, c = place()
    colour = lax.rem(y + z, 2)
    partner = {"s": 2 * x + (1 - c)}
    across = {"s": 2 * (1 - x) + c}
    beside = ({"r": lax.rem(r + 4, 8)}, {"r": r + 1 - 2 * lax.rem(z, 2)})
    mine, theirs, others = 2 * x + c, 2 * (1 - x) + c, 2 * (1 - x) + (1 - c)
    shards = (wg_in, wu_in, wd_in)
    whole = (wg_v, wu_v, wd_v, w1g, w1u, w1d)
    rows = (192, 192, 448, 192, 192, 448)

    def piece(m, q, half, k):
        n = rows[m] // 4
        return whole[m].at[pl.ds(pl.multiple_of(q * rows[m] + half * (2 * n) + k * n, 16), n)]

    def quarter(m, q):
        return whole[m].at[pl.ds(pl.multiple_of(q * rows[m], 16), rows[m])]

    def remote(src, dst, send, recv, to):
        return pltpu.make_async_remote_copy(src_ref=src, dst_ref=dst, send_sem=send, recv_sem=recv, device_id=to, device_id_type=MESH)

    def first(m, k):
        n = rows[m] // 4
        src = shards[m % 3].at[m // 3, pl.ds(pl.multiple_of(colour * (2 * n) + k * n, 16), n)]
        return remote(src, piece(m, mine, colour, k), sa_s.at[m, k], sa_r.at[m, k], across)

    def own(m):
        return remote(shards[m % 3].at[m // 3], quarter(m, mine), so_s.at[m], so_r.at[m], partner)

    def relay(m, k):
        p = piece(m, theirs, colour, k)
        return remote(p, p, sr_s.at[m, k], sr_r.at[m, k], beside[k])

    def pass_on(m, j, k):
        p = piece(m, theirs, colour if j == 0 else 1 - colour, k)
        return remote(p, p, sp_s.at[m, j, k], sp_r.at[m, j, k], partner)

    def arrived(copy):
        copy.wait_recv()

    def at_first(m, k):
        remote(piece(m, theirs, colour, k), piece(m, theirs, colour, k), sa_s.at[m, k], sa_r.at[m, k], across).wait_recv()
        relay(m, k).start()
        pass_on(m, 0, k).start()

    def at_beside(m, k):
        p = piece(m, theirs, 1 - colour, k)
        remote(p, p, sr_s.at[m, k], sr_r.at[m, k], beside[k]).wait_recv()
        pass_on(m, 1, k).start()

    def at_end(m):
        q = quarter(m, 2 * x + (1 - c))
        remote(q, q, so_s.at[m], so_r.at[m], partner).wait_recv()
        for j in range(2):
            for k in range(2):
                p = piece(m, others, colour if j == 0 else 1 - colour, k)
                remote(p, p, sp_s.at[m, j, k], sp_r.at[m, j, k], partner).wait_recv()

    barrier = pltpu.get_barrier_semaphore()
    for to in (partner, across, *beside):
        pl.semaphore_signal(barrier, inc=1, device_id=to, device_id_type=MESH)

    loads = []
    for m in range(3):
        loads.append(pltpu.make_async_copy(shards[m].at[0], quarter(m, mine), s_loc.at[m]))
        loads.append(pltpu.make_async_copy(shards[m].at[1], (og, ou, od)[m], s_loc.at[3 + m]))
    for copy in loads:
        copy.start()

    def load_h(i):
        return pltpu.make_async_copy(x_hbm.at[pl.ds(i * T, T)], hin.at[lax.rem(i, 2)], s_hin.at[lax.rem(i, 2)])

    load_h(0).start()
    pl.semaphore_wait(barrier, 4)
    for m in range(6):
        for k in range(2):
            first(m, k).start()
        own(m).start()

    def store_at(i):
        return pltpu.make_async_copy(at_s.at[lax.rem(i, 2)], at_hbm.at[:, pl.ds(pl.multiple_of(i * T, T), T)], s_at.at[lax.rem(i, 2)])

    @pl.loop(0, 8)
    def _(i):
        load_h(i).wait()

        @pl.when(i < 7)
        def _():
            load_h(i + 1).start()

        @pl.when(i >= 2)
        def _():
            store_at(i - 2).wait()

        h = hin[lax.rem(i, 2)].astype(F32)
        a = (h * lax.rsqrt(jnp.mean(h * h, -1, keepdims=True) + 1e-6)).astype(BF)
        a_v[pl.ds(i * T, T)] = a
        at_s[lax.rem(i, 2)] = a.T
        store_at(i).start()

    store_at(6).wait()
    store_at(7).wait()
    for copy in loads:
        copy.wait()
    saves = [pltpu.make_async_copy((og, ou, od)[m], quarter(3 + m, mine), s_loc.at[m]) for m in range(3)]
    for copy in saves:
        copy.start()

    for k in range(2):
        at_first(0, k)
    for k in range(2):
        at_beside(0, k)
    at_end(0)

    w0_out = [pltpu.make_async_copy(whole[m], (w0g, w0u, w0d)[m], s_w0.at[m]) for m in range(3)]
    w0_out[0].start()

    def store_gate(i):
        return pltpu.make_async_copy(gate_v.at[pl.ds(i * T, T)], gate_hbm.at[pl.ds(i * T, T)], s_gate.at[i])

    ACTS1 = {0: [(at_first, 1, 0)], 2: [(at_first, 1, 1)], 4: [(at_beside, 1, 0), (at_first, 2, 0)], 6: [(at_beside, 1, 1), (at_first, 2, 1)]}
    ACTS2 = {0: [(at_beside, 2, 0), (at_beside, 2, 1), (at_first, 3, 0), (at_first, 3, 1)], 2: [(at_beside, 3, 0), (at_first, 4, 0)],
             3: [(at_beside, 3, 1), (at_first, 4, 1)], 4: [(at_beside, 4, 0), (at_first, 5, 0)], 5: [(at_beside, 4, 1), (at_first, 5, 1)],
             6: [(at_beside, 5, 0)], 7: [(at_beside, 5, 1)]}

    def act(acts, i):
        for step, todo in acts.items():
            @pl.when(i == step)
            def _():
                for f, m, k in todo:
                    f(m, k)

    @pl.loop(0, 8)
    def _(i):
        act(ACTS1, i)
        for half in range(2):
            rs = pl.ds(pl.multiple_of(i * T + half * (T // 2), T // 2), T // 2)
            a = a_v[rs]
            for n in range(7):
                gate_v[rs, n * 256:(n + 1) * 256] = dot(a, wg_v[:, n * 256:(n + 1) * 256])
        store_gate(i).start()

    at_end(1)
    w0_out[1].start()

    def store_up(i):
        return pltpu.make_async_copy(up_s.at[lax.rem(i, 2)], up_hbm.at[pl.ds(i * T, T)], s_up.at[lax.rem(i, 2)])

    def store_h1(i):
        return pltpu.make_async_copy(h1_s.at[lax.rem(i, 2)], h1_hbm.at[pl.ds(i * T, T)], s_h1.at[lax.rem(i, 2)])

    load_h(0).start()

    @pl.loop(0, 8)
    def _(i):
        act(ACTS2, i)
        load_h(i).wait()

        @pl.when(i < 7)
        def _():
            load_h(i + 1).start()

        @pl.when(i >= 2)
        def _():
            store_up(i - 2).wait()
            store_h1(i - 2).wait()

        @pl.when(i == 0)
        def _():
            at_end(2)
            w0_out[2].start()

        slot = lax.rem(i, 2)
        for half in range(2):
            lo = half * (T // 2)
            rs = pl.ds(pl.multiple_of(i * T + lo, T // 2), T // 2)
            a = a_v[rs]
            for n in range(7):
                cs = slice(n * 256, (n + 1) * 256)
                g = gate_v[rs, cs]
                u = dot(a, wu_v[:, cs])
                up_s[slot, lo:lo + T // 2, cs] = u
                hid_s[lo:lo + T // 2, cs] = (g * sigmoid(g) * u).astype(BF)
        for half in range(2):
            lo = half * (T // 2)
            o = dot(hid_s[lo:lo + T // 2], wd_v[...]).astype(BF)
            h1_s[slot, lo:lo + T // 2] = hin[slot, lo:lo + T // 2] + o
        store_up(i).start()
        store_h1(i).start()

    for m in range(3, 6):
        at_end(m)
    for i in (6, 7):
        store_up(i).wait()
        store_h1(i).wait()
    for i in range(8):
        store_gate(i).wait()
    for copy in w0_out + saves:
        copy.wait()
    for m in range(6):
        own(m).wait_send()
        for k in range(2):
            first(m, k).wait_send()
            relay(m, k).wait_send()
            for j in range(2):
                pass_on(m, j, k).wait_send()


def forward(x, wg, wu, wd):
    S = jax.ShapeDtypeStruct
    dma = pltpu.SemaphoreType.DMA
    return pl.pallas_call(
        forward_kernel,
        out_shape=(S((TOK, D), BF), S((TOK, FF), F32), S((TOK, FF), F32), S((D, TOK), BF),
                   S((D, FF), BF), S((D, FF), BF), S((FF, D), BF), S((D, FF), BF), S((D, FF), BF), S((FF, D), BF)),
        in_specs=[ANY] * 4,
        out_specs=(ANY,) * 10,
        scratch_shapes=[
            pltpu.VMEM((D, FF), BF), pltpu.VMEM((D, FF), BF), pltpu.VMEM((FF, D), BF),
            pltpu.VMEM((192, FF), BF), pltpu.VMEM((192, FF), BF), pltpu.VMEM((448, D), BF),
            pltpu.VMEM((TOK, D), BF), pltpu.VMEM((TOK, FF), F32),
            pltpu.VMEM((2, T, D), BF), pltpu.VMEM((2, T, FF), F32), pltpu.VMEM((2, D, T), BF),
            pltpu.VMEM((T, FF), BF), pltpu.VMEM((2, T, D), BF),
            dma((6, 2)), dma((6, 2)), dma((6, 2)), dma((6, 2)), dma((6, 2, 2)), dma((6, 2, 2)), dma((6,)), dma((6,)),
            dma((6,)), dma((2,)), dma((2,)), dma((2,)), dma((2,)), dma((8,)), dma((3,)),
        ],
        compiler_params=pltpu.CompilerParams(collective_id=0, has_side_effects=True, vmem_limit_bytes=67_000_000),
        cost_estimate=pl.CostEstimate(flops=6 * TOK * D * FF, bytes_accessed=120_000_000, transcendentals=TOK * FF),
        name="forward",
    )(x, wg, wu, wd)


def full(shape):
    return pl.BlockSpec(shape, lambda i: (0,) * len(shape), pipeline_mode=pl.Buffered(1))


def tile(t, n):
    return pl.BlockSpec((t, n), lambda i: (i, 0))


def norm_back(da, h, dy):
    h, da = h.astype(F32), da.astype(BF).astype(F32)
    scale = lax.rsqrt(jnp.mean(h * h, -1, keepdims=True) + 1e-6)
    along = jnp.sum(da * h, -1, keepdims=True) * (scale * scale * scale * (1.0 / D))
    return dy + (da * scale - h * along).astype(BF)


def last_kernel(h_ref, dy_ref, wg, wu, wd, dh_ref, dg_ref, du_ref, dwd, at_ref, a_s, hid_s):
    n_rows = h_ref.shape[0]
    for lo in range(0, n_rows, 512):
        r = slice(lo, lo + 512)
        h = h_ref[r].astype(F32)
        a_s[r] = (h * lax.rsqrt(jnp.mean(h * h, -1, keepdims=True) + 1e-6)).astype(BF)
    for lo in range(0, n_rows, 512):
        r = slice(lo, lo + 512)
        for n in range(7):
            cs = slice(n * 256, (n + 1) * 256)
            g, u = dot(a_s[r], wg[:, cs]), dot(a_s[r], wu[:, cs])
            back = dot_nt(dy_ref[r], wd[cs]).astype(BF).astype(F32)
            s = sigmoid(g)
            silu = g * s
            hid_s[r, cs] = (silu * u).astype(BF)
            dg_ref[r, cs] = (back * u * (s + silu * (1 - s))).astype(BF)
            du_ref[r, cs] = (back * silu).astype(BF)
    for lo in range(0, n_rows, 256):
        r = slice(lo, lo + 256)
        dh_ref[r] = norm_back(dot_nt(dg_ref[r], wg[...]) + dot_nt(du_ref[r], wu[...]), h_ref[r], dy_ref[r])
    at_ref[...] = a_s[...].T

    @pl.when(pl.program_id(0) == 0)
    def _():
        dwd[...] = jnp.zeros_like(dwd)

    dwd[...] += dot_tn(hid_s[...], dy_ref[...])


def last_layer(h, dy, wg, wu, wd, t=1024):
    S = jax.ShapeDtypeStruct
    return pl.pallas_call(
        last_kernel,
        grid=(TOK // t,),
        in_specs=[tile(t, D), tile(t, D), full((D, FF)), full((D, FF)), full((FF, D))],
        out_specs=[tile(t, D), tile(t, FF), tile(t, FF), full((FF, D)), pl.BlockSpec((D, t), lambda i: (0, i))],
        out_shape=[S((TOK, D), BF), S((TOK, FF), BF), S((TOK, FF), BF), S((FF, D), F32), S((D, TOK), BF)],
        scratch_shapes=[pltpu.VMEM((t, D), BF), pltpu.VMEM((t, FF), BF)],
        compiler_params=pltpu.CompilerParams(vmem_limit_bytes=66_000_000),
        cost_estimate=pl.CostEstimate(flops=12 * TOK * D * FF, bytes_accessed=80_000_000, transcendentals=TOK * FF),
        name="last_layer",
    )(h, dy, wg, wu, wd)


def hidden_kernel(gate_ref, up_ref, dy_ref, wd, dg_ref, du_ref, dwd, hid_s):
    for lo in range(0, 512, 256):
        r = slice(lo, lo + 256)
        for n in range(7):
            cs = slice(n * 256, (n + 1) * 256)
            back = dot_nt(dy_ref[r], wd[cs]).astype(BF).astype(F32)
            g, u = gate_ref[r, cs], up_ref[r, cs]
            s = sigmoid(g)
            silu = g * s
            hid_s[r, cs] = (silu * u).astype(BF)
            dg_ref[r, cs] = (back * u * (s + silu * (1 - s))).astype(BF)
            du_ref[r, cs] = (back * silu).astype(BF)

    @pl.when(pl.program_id(0) == 0)
    def _():
        dwd[...] = jnp.zeros_like(dwd)

    for lo in range(0, FF, FF // 2):
        r = slice(lo, lo + FF // 2)
        dwd[r] += dot_tn(hid_s[:, r], dy_ref[...])


def hidden_back(gate, up, dy, wd, t=512):
    S = jax.ShapeDtypeStruct
    return pl.pallas_call(
        hidden_kernel,
        grid=(TOK // t,),
        in_specs=[tile(t, FF), tile(t, FF), tile(t, D), full((FF, D))],
        out_specs=[tile(t, FF), tile(t, FF), full((FF, D))],
        out_shape=[S((TOK, FF), BF), S((TOK, FF), BF), S((FF, D), F32)],
        scratch_shapes=[pltpu.VMEM((t, FF), BF)],
        compiler_params=pltpu.CompilerParams(vmem_limit_bytes=66_000_000),
        cost_estimate=pl.CostEstimate(flops=4 * TOK * D * FF, bytes_accessed=100_000_000, transcendentals=TOK * FF),
        name="hidden_back",
    )(gate, up, dy, wd)


def weight_kernel(at, d_ref, o_ref):
    o_ref[...] = dot(at[...], d_ref[...]).astype(BF)


def weight_back(at, d):
    return pl.pallas_call(
        weight_kernel,
        grid=(7,),
        in_specs=[full((D, TOK)), pl.BlockSpec((TOK, 256), lambda i: (0, i))],
        out_specs=pl.BlockSpec((D, 256), lambda i: (0, i)),
        out_shape=jax.ShapeDtypeStruct((D, FF), BF),
        compiler_params=pltpu.CompilerParams(vmem_limit_bytes=40_000_000),
        cost_estimate=pl.CostEstimate(flops=2 * TOK * D * FF, bytes_accessed=22_000_000, transcendentals=0),
        name="weight_back",
    )(at, d)


def input_kernel(dg, du, wg, wu, h_ref, dy_ref, o_ref):
    for lo in range(0, h_ref.shape[0], 256):
        r = slice(lo, lo + 256)
        o_ref[r] = norm_back(dot_nt(dg[r], wg[...]) + dot_nt(du[r], wu[...]), h_ref[r], dy_ref[r])


def input_back(dg, du, wg, wu, h, dy, t=1024):
    return pl.pallas_call(
        input_kernel,
        grid=(TOK // t,),
        in_specs=[tile(t, FF), tile(t, FF), full((D, FF)), full((D, FF)), tile(t, D), tile(t, D)],
        out_specs=tile(t, D),
        out_shape=jax.ShapeDtypeStruct((TOK, D), BF),
        compiler_params=pltpu.CompilerParams(vmem_limit_bytes=60_000_000),
        cost_estimate=pl.CostEstimate(flops=4 * TOK * D * FF, bytes_accessed=60_000_000, transcendentals=0),
        name="input_back",
    )(dg, du, wg, wu, h, dy)


def solution(mesh):
    def summed(term):
        return lax.psum(lax.psum_scatter(term, "s", scatter_dimension=0, tiled=True), "r")

    def step(x, dy, wg, wu, wd):
        x, dy = x[0], dy[0]
        h1, gate, up, at0, w0g, w0u, w0d, w1g, w1u, w1d = forward(x, wg, wu, wd)
        dh, dg1, du1, dwd1, at1 = last_layer(h1, dy, w1g, w1u, w1d)
        by1 = [summed(t) for t in (weight_back(at1, dg1), weight_back(at1, du1), dwd1.astype(BF))]
        dg0, du0, dwd0 = hidden_back(gate, up, dh, w0d)
        by0 = [summed(t) for t in (weight_back(at0, dg0), weight_back(at0, du0), dwd0.astype(BF))]
        by_x = input_back(dg0, du0, w0g, w0u, x, dh)
        return (by_x[None], *(jnp.stack([a, b]) for a, b in zip(by0, by1)))

    states, cut = P(("rep", "r", "s"), None, None), P(None, "s", None)
    return jax.shard_map(
        step,
        mesh=mesh,
        in_specs=(states, states) + (cut,) * 3,
        out_specs=(states,) + (P("rep", "s", None),) * 3,
        check_vma=False,
    )
```

time: 705 us -> 576 us (0.82); the launches traced: 698 us -> 577 us
  matrix products: 414 us -> 0 us
  Pallas kernels: 0 us -> 294 us
  waiting for transfers between devices: 205 us -> 244 us
  local copies, waits for them, and re-layouts: 34 us -> 11.1 us
  other arithmetic: 29.1 us -> 13.2 us
    dot_general x17 -> x0, matrix products: 414 us -> none  [the longest x6 149 us: layer(): up = jnp.dot(a, w['w_up'], preferred_element_type=jnp.float32)]
    pallas_call x0 -> x8, Pallas kernels: none -> 294 us  [the longest x1 92.6 us: last_layer(): pl.pallas_call(last_kernel, grid=(TOK // t,), in_specs=[tile(t, D), tile(...]
    reduce_scatter x6, waiting for transfers between devices: 61.8 us -> 120 us  [summed(): lax.psum_scatter(term, 's', scatter_dimension=0, tiled=True)]
    all_gather x6 -> x0, waiting for transfers between devices: 28.4 us -> none  [fetched(): lax.all_gather(w[number], 's', axis=0, tiled=True)]
    unnamed x27 -> x16, local copies, waits for them, and re-layouts: 26.6 us -> 11.1 us
    psum x1, waiting for transfers between devices: 113 us -> 124 us  [summed(): lax.psum(lax.psum_scatter(term, 's', scatter_dimension=0, tiled=True), 'r')]
    add_any x1 -> x0, other arithmetic: 9.5 us -> none  [normed(): wide = h.astype(jnp.float32)]
    broadcast_in_dim x1 -> x0, other arithmetic: 9.5 us -> none  [step(): by_h[None]]
  transfers between devices with their start and end apart: 13 -> 7, of which waited for: 8 -> 5; matrix products, arithmetic and copies ran while one was open for 51% -> 2% of each run, Pallas kernels for 0% -> 21%
where the time goes in v1:
time: 576 us; the launch traced here: 577 us
  Pallas kernels  294 us (51%)
  waiting for transfers between devices  244 us (42%)
  between operations  14.7 us (3%)
  other arithmetic  13.2 us (2%)
  local copies, waits for them, and re-layouts  11.1 us (2%)
    psum x1, waiting for transfers between devices, summed(): lax.psum(lax.psum_scatter(term, 's', scatter_dimension=0, tiled=True), 'r')  124 us
    reduce_scatter x6, waiting for transfers between devices, summed(): lax.psum_scatter(term, 's', scatter_dimension=0, tiled=True)  120 us
    pallas_call x1, Pallas kernels, last_layer(): pl.pallas_call(last_kernel, grid=(TOK // t,), in_specs=[tile(t, D), tile(...  92.6 us
    pallas_call x1, Pallas kernels, forward(): pl.pallas_call(forward_kernel, out_shape=(S((TOK, D), BF), S((TOK, FF), F...  65.9 us
    pallas_call x4, Pallas kernels, weight_back(): pl.pallas_call(weight_kernel, grid=(7,), in_specs=[full((D, TOK)), pl.Blo...  60.5 us
    pallas_call x1, Pallas kernels, hidden_back(): pl.pallas_call(hidden_kernel, grid=(TOK // t,), in_specs=[tile(t, FF), ti...  40.4 us
    pallas_call x1, Pallas kernels, input_back(): pl.pallas_call(input_kernel, grid=(TOK // t,), in_specs=[tile(t, FF), til...  34.1 us
  transfers between devices with their start and end apart: 7, of which 5 were waited for; matrix products, arithmetic and copies ran while one was open for 2% of the time, Pallas kernels for 21%

profile of v1, /device:TPU:0, one launch (start us, length us, event | category | flops | bytes accessed | tf_op | source)
XLA Modules:
  0.0 576.8 jit_solution(15767376242552899056)
XLA Ops:
  7.2 65.9 %forward.1 = (bf16[4096,768]{1,0:T(8,128)(2,1)}, f32[4096,1792]{1,0:T(8,128)}, f32[4096,1792]{1,0:T(8,128)}, bf16[768,4096]{1,0:T(8,128)(2,1)}, bf16[768,1792]{1...) custom-call(bf16[4096,768]{1,0:T(8,128)(2,1)} %bitcast.16, ...), custom_call_target="tpu_custom_call" | custom-call | flops 33822867456 | bytes 120000000 | tf_op jit(solution)/shard_map/forward/pallas_call | solution.py:251
  73.1 92.6 %last_layer.1 = (bf16[4096,768]{1,0:T(8,128)(2,1)}, bf16[4096,1792]{1,0:T(8,128)(2,1)}, bf16[4096,1792]{1,0:T(8,128)(2,1)}, f32[1792,768]{1,0:T(8,128)}, bf16[768,4096]{1,0:T(8,128)(2,1)}) custom-call(bf16[4096,768]{1,0:T(8,128)(2,1)} %get-tuple-element.24.h_ref, bf16[4096,768]{1,0:T(8,128)(2,1)} %bitcast.15, bf16[768,1792]{1,0:T(8,128)(2,1)} %get-tuple-element.25.wg, ...), custom_call_target="tpu_custom_call" | custom-call | flops 67645734912 | bytes 80000000 | tf_op jit(solution)/shard_map/last_layer/pallas_call | solution.py:318
  165.8 2.8 copy-done.2
  168.5 15.2 %weight_back.7 = bf16[768,1792]{1,0:T(8,128)(2,1)} custom-call(bf16[768,4096]{1,0:T(8,128)(2,1)S(1)} %copy-done.2, bf16[4096,1792]{1,0:T(8,128)(2,1)} %get-tuple-element.37.d_ref), custom_call_target="tpu_custom_call" | custom-call | flops 11274289152 | bytes 22000000 | tf_op jit(solution)/shard_map/weight_back/pallas_call | solution.py:373
  183.8 2.8 copy-done.3
  186.6 15.1 %weight_back.5 = bf16[768,1792]{1,0:T(8,128)(2,1)} custom-call(bf16[768,4096]{1,0:T(8,128)(2,1)S(1)} %copy-done.3, bf16[4096,1792]{1,0:T(8,128)(2,1)} %get-tuple-element.36.d_ref), custom_call_target="tpu_custom_call" | custom-call | flops 11274289152 | bytes 22000000 | tf_op jit(solution)/shard_map/weight_back/pallas_call | solution.py:373
  201.8 40.4 %hidden_back.1 = (bf16[4096,1792]{1,0:T(8,128)(2,1)}, bf16[4096,1792]{1,0:T(8,128)(2,1)}, f32[1792,768]{1,0:T(8,128)}) custom-call(f32[4096,1792]{1,0:T(8,128)} %get-tuple-element.22.gate_ref, f32[4096,1792]{1,0:T(8,128)} %get-tuple-element.23.up_ref, bf16[4096,768]{1,0:T(8,128)(2,1)} %get-tuple-element.28.dy_ref, bf16[1792,768]{1,0:T(8,128)(2,1)} %get-tuple-element.29.wd), custom_call_target="tpu_custom_call" | custom-call | flops 22548578304 | bytes 100000000 | tf_op jit(solution)/shard_map/hidden_back/pallas_call | solution.py:355
  242.2 4.4 convert_element_type.6
  246.6 0.0 reduce-scatter.7.cloned.1.call-start
  246.6 2.8 copy-done
  249.4 15.1 %weight_back.4 = bf16[768,1792]{1,0:T(8,128)(2,1)} custom-call(bf16[768,4096]{1,0:T(8,128)(2,1)S(1)} %copy-done, bf16[4096,1792]{1,0:T(8,128)(2,1)} %get-tuple-element.30.dg.d_ref), custom_call_target="tpu_custom_call" | custom-call | flops 11274289152 | bytes 22000000 | tf_op jit(solution)/shard_map/weight_back/pallas_call | solution.py:373
  264.5 0.0 reduce-scatter.11.cloned.1.call-start
  264.6 2.8 copy-done.1
  267.3 15.2 %weight_back.6 = bf16[768,1792]{1,0:T(8,128)(2,1)} custom-call(bf16[768,4096]{1,0:T(8,128)(2,1)S(1)} %copy-done.1, bf16[4096,1792]{1,0:T(8,128)(2,1)} %get-tuple-element.31.du.d_ref), custom_call_target="tpu_custom_call" | custom-call | flops 11274289152 | bytes 22000000 | tf_op jit(solution)/shard_map/weight_back/pallas_call | solution.py:373
  282.5 0.0 reduce-scatter.17.cloned.1.call-start
  282.6 4.4 convert_element_type.7
  287.1 7.2 %reduce-scatter.15.cloned.1.call-done = bf16[448,768]{1,0:T(8,128)(2,1)} async-done(((bf16[1792,768]{1,0:T(8,128)(2,1)}), bf16[448,768]{1,0:T(8,128)(2,1)}) %reduce-scatter.15.cloned.1.call-update) | async-done | bytes 688144 | tf_op jit(solution)/shard_map/reduce_scatter | solution.py:406
  294.2 38.1 %reduce-scatter.7.cloned.1.call-done = bf16[192,1792]{1,0:T(8,128)(2,1)} async-done(((bf16[768,1792]{1,0:T(8,128)(2,1)}), bf16[192,1792]{1,0:T(8,128)(2,1)}) %reduce-scatter.7.cloned.1.call-update) | async-done | bytes 688144 | tf_op jit(solution)/shard_map/reduce_scatter | solution.py:406
  332.3 37.5 %reduce-scatter.11.cloned.1.call-done = bf16[192,1792]{1,0:T(8,128)(2,1)} async-done(((bf16[768,1792]{1,0:T(8,128)(2,1)}), bf16[192,1792]{1,0:T(8,128)(2,1)}) %reduce-scatter.11.cloned.1.call-update) | async-done | bytes 688144 | tf_op jit(solution)/shard_map/reduce_scatter | solution.py:406
  369.8 37.5 %reduce-scatter.17.cloned.1.call-done = bf16[448,768]{1,0:T(8,128)(2,1)} async-done(((bf16[1792,768]{1,0:T(8,128)(2,1)}), bf16[448,768]{1,0:T(8,128)(2,1)}) %reduce-scatter.17.cloned.1.call-update) | async-done | bytes 688144 | tf_op jit(solution)/shard_map/reduce_scatter | solution.py:406
  407.4 34.1 %input_back.1 = bf16[4096,768]{1,0:T(8,128)(2,1)} custom-call(bf16[4096,1792]{1,0:T(8,128)(2,1)} %get-tuple-element.30.dg.d_ref, bf16[4096,1792]{1,0:T(8,128)(2,1)} %get-tuple-element.31.du.d_ref, bf16[768,1792]{1,0:T(8,128)(2,1)} %get-tuple-element.32.wg, bf16[768,1792]{1,0:T(8,128)(2,1)} %get-tuple-element.33.wu, bf16[4096,768]{1,0:T(8,128)(2,1)} %bitcast.17, ...), custom_call_target="tpu_custom_call" | custom-call | flops 22548578304 | bytes 60000000 | tf_op jit(solution)/shard_map/input_back/pallas_call | solution.py:392
  441.5 123.5 %all-reduce.3.cloned.1.call-done = (bf16[1,192,1792]{2,1,0:T(8,128)(2,1)}, bf16[1,192,1792]{2,1,0:T(8,128)(2,1)}, bf16[1,192,1792]{2,1,0:T(8,128)(2,1)}, bf16[1,...) async-done(((bf16[1,192,1792]{2,1,0:T(8,128)(2,1)}, bf16[1,192,1792]{2,1,0:T(8,128)(2,1)}, bf16[1,192,1792]{2,1,0:T(8,128)(2,1)}, ...) | async-done | bytes 4128784 | tf_op jit(solution)/shard_map/psum | solution.py:406
  565.1 2.7 pad_maximum_fusion.2
  567.7 1.8 pad_maximum_fusion
  (25 shorter events, 0.3 us)
Async XLA Ops:
  7.2 279.9 %reduce-scatter.13.cloned.1.call-start = ((), (), s32[]{:S(2)}) async-start(), calls=%async_computation.9 | async-start | bytes 3440640 | tf_op jit(solution)/shard_map/reduce_scatter | solution.py:406
  165.8 2.8 copy-start.2
  183.8 103.3 %reduce-scatter.9.cloned.1.call-start = ((), (), s32[]{:S(2)}) async-start(), calls=%async_computation.7 | async-start | bytes 3440640 | tf_op jit(solution)/shard_map/reduce_scatter | solution.py:406
  183.8 2.8 copy-start.3
  201.7 92.5 %reduce-scatter.15.cloned.1.call-start = ((), (), s32[]{:S(2)}) async-start(), calls=%async_computation.10 | async-start | bytes 3440640 | tf_op jit(solution)/shard_map/reduce_scatter | solution.py:406
  246.6 85.8 %reduce-scatter.7.cloned.1.call-start = ((), (), s32[]{:S(2)}) async-start(), calls=%async_computation.6 | async-start | bytes 3440640 | tf_op jit(solution)/shard_map/reduce_scatter | solution.py:406
  246.6 2.8 copy-start
  264.5 105.3 %reduce-scatter.11.cloned.1.call-start = ((), (), s32[]{:S(2)}) async-start(), calls=%async_computation.8 | async-start | bytes 3440640 | tf_op jit(solution)/shard_map/reduce_scatter | solution.py:406
  264.6 2.8 copy-start.1
  282.5 124.8 %reduce-scatter.17.cloned.1.call-start = ((), (), s32[]{:S(2)}) async-start(), calls=%async_computation.11 | async-start | bytes 3440640 | tf_op jit(solution)/shard_map/reduce_scatter | solution.py:406
  287.0 278.1 %all-reduce.3.cloned.1.call-start = ((), (), s32[]{:S(2)}) async-start(), calls=%async_computation.12 | async-start | bytes 8257536 | tf_op jit(solution)/shard_map/psum | solution.py:406
  565.0 2.7 copy-start.4
  565.1 2.7 copy-start.5
  565.1 2.7 copy-start.6
  565.1 2.7 copy-start.7
Sparse Core Ops, SparseCore 0:
  183.9 34.9 reduce-scatter.12
  221.5 35.0 reduce-scatter.8
  259.1 35.0 reduce-scatter.14
  297.2 35.0 reduce-scatter.6
  334.7 35.0 reduce-scatter.10
  372.3 35.0 reduce-scatter.16
  411.7 153.3 all-reduce.2

commit v2 on v0

v2 whole, which is shorter than its diff:
```python
import functools
import jax
import jax.numpy as jnp
from jax import lax
from jax.experimental import pallas as pl
from jax.experimental.pallas import tpu as pltpu
from jax.sharding import PartitionSpec as P

F32, BF = jnp.float32, jnp.bfloat16
TOK, D, FF = 4096, 768, 1792
B = 256
NF = FF // B
TILES = 8
T = TOK // TILES
ANY = pl.BlockSpec(memory_space=pl.ANY)
DMA = pltpu.SemaphoreType.DMA
VMEM_LIMIT = 67_000_000


def dot(a, b):
    return jnp.dot(a, b, preferred_element_type=F32)


def dot_nt(a, b):
    return lax.dot_general(a, b, (((1,), (1,)), ((), ())), preferred_element_type=F32)


def sigmoid(g):
    return 0.5 + 0.5 * jnp.tanh(0.5 * g)


def odd(i):
    return lax.rem(i, 2)


def span(i, n, unit=None):
    return pl.ds(pl.multiple_of(i * n, unit or n), n)


def columns(n):
    return slice(n * B, (n + 1) * B)


def go(copies):
    for copy in copies:
        copy.start()


def done(copies):
    for copy in copies:
        copy.wait()


def local(src, dst, sem):
    return pltpu.make_async_copy(src, dst, sem)


def remote(src, dst, send, recv, to):
    return pltpu.make_async_remote_copy(src_ref=src, dst_ref=dst, send_sem=send, recv_sem=recv, device_id=to, device_id_type=pl.DeviceIdType.MESH)


def meet(peers):
    barrier = pltpu.get_barrier_semaphore()
    for to in peers:
        pl.semaphore_signal(barrier, inc=1, device_id=to, device_id_type=pl.DeviceIdType.MESH)
    return lambda: pl.semaphore_wait(barrier, len(peers))


def place():
    r, s = lax.axis_index("r"), lax.axis_index("s")
    return r // 4, lax.rem(r, 4), s // 2, odd(s)


def in_quad(y, z):
    return {"r": 4 * y + z}


def on_core(x, c):
    return {"s": 2 * x + c}


PARTS = (3, 3, 1, 1, 1, 1)


def forward_kernel(x_hbm, wg_in, wu_in, wd_in,
                   h1_hbm, gate_hbm, up_hbm, at_hbm, hidt_hbm, w0g, w0u, w0d, w1g, w1u, w1d,
                   wg_v, wu_v, wd_v, og, ou, od, a_v, gate_v, hin, up_s, at_s, hid_s, hidt_s, h1_s,
                   sa, sr, sp, sq, so, s_loc, s_hin, s_up, s_at, s_h1, s_gate, s_w0, s_hidt):
    y, z, x, c = place()
    colour = odd(y + z)
    partner, across = on_core(x, 1 - c), on_core(1 - x, c)
    beside = in_quad(1 - y, z), in_quad(y, z + 1 - 2 * odd(z))
    mine, theirs, others = 2 * x + c, 2 * (1 - x) + c, 2 * (1 - x) + 1 - c
    shards = wg_in, wu_in, wd_in
    whole = wg_v, wu_v, wd_v, w1g, w1u, w1d
    rows = tuple(ref.shape[0] // 4 for ref in whole)

    def piece(m, q, half, way, k):
        n = rows[m] // (4 * PARTS[m])
        return span((2 * half + way) * PARTS[m] + k, n, 16), span((4 * q + 2 * half + way) * PARTS[m] + k, n, 16)

    def quarter(m, q):
        return whole[m].at[span(q, rows[m])]

    def sems(table, m, way, k):
        at = 2 * (sum(PARTS[:m]) + k) + way
        return table.at[0, at], table.at[1, at]

    def first(m, way, k):
        src, dst = piece(m, mine, colour, way, k)
        return remote(shards[m % 3].at[m // 3, src], whole[m].at[dst], *sems(sa, m, way, k), across)

    def own(m):
        return remote(shards[m % 3].at[m // 3], quarter(m, mine), so.at[0, m], so.at[1, m], partner)

    def onward(m, q, half, way, k, table, to):
        p = whole[m].at[piece(m, q, half, way, k)[1]]
        return remote(p, p, *sems(table, m, way, k), to)

    def relay(m, way, k):
        return onward(m, theirs, colour, way, k, sr, beside[way])

    def pass_first(m, way, k):
        return onward(m, theirs, colour, way, k, sp, partner)

    def pass_beside(m, way, k):
        return onward(m, theirs, 1 - colour, way, k, sq, partner)

    def every(m):
        return [(m, way, k) for k in range(PARTS[m]) for way in range(2)]

    def at_first(m, way, k):
        onward(m, theirs, colour, way, k, sa, across).wait_recv()
        relay(m, way, k).start()
        pass_first(m, way, k).start()

    def at_beside(m, way, k):
        onward(m, theirs, 1 - colour, way, k, sr, beside[way]).wait_recv()
        pass_beside(m, way, k).start()

    def at_end(m):
        for p in every(m):
            pass_first(*p).wait_recv()
            pass_beside(*p).wait_recv()

    def all_of(f, *matrices):
        for m in matrices:
            for p in every(m):
                f(*p)

    met = meet((partner, across, *beside))
    loads = [local(shards[m].at[n], (quarter(m, mine), (og, ou, od)[m])[n], s_loc.at[n, m]) for n in range(2) for m in range(3)]
    go(loads)

    def load_h(i):
        return local(x_hbm.at[span(i, T)], hin.at[odd(i)], s_hin.at[odd(i)])

    def next_h(i):
        load_h(i).wait()

        @pl.when(i < TILES - 1)
        def _():
            load_h(i + 1).start()

    takes = [local(x_hbm.at[span(i, T)], a_v.at[span(i, T)], s_gate.at[i]) for i in range(TILES)]
    go(takes)
    met()
    for m in range(6):
        own(m).start()
        all_of(lambda *p: first(*p).start(), m)

    @pl.loop(0, TILES)
    def _(i):
        local(x_hbm.at[span(i, T)], a_v.at[span(i, T)], s_gate.at[i]).wait()
        h = a_v[span(i, T)].astype(F32)
        a_v[span(i, T)] = (h * lax.rsqrt(jnp.mean(h * h, -1, keepdims=True) + 1e-6)).astype(BF)

    done(loads)
    saves = [local((og, ou, od)[m], quarter(3 + m, mine), s_loc.at[0, m]) for m in range(3)]
    go(saves)
    own(0).wait_recv()
    order = every(0)

    def in_turn(i, todo):
        for step, work in enumerate(todo):
            @pl.when(i == step)
            def _():
                for f, *p in work:
                    f(*p)

    def halves(i):
        return [span(2 * i + half, T // 2) for half in range(2)]

    @pl.loop(0, TILES)
    def _(i):
        in_turn(i - 1, [[(at_first, *p)] for p in order])
        ks = span(2 * x, B)
        for rs in halves(i):
            for n in range(NF):
                gate_v[rs, columns(n)] = dot(a_v[rs, ks], wg_v[ks, columns(n)])

    all_of(at_beside, 0)
    all_of(at_first, 1)
    at_end(0)
    w0_out = [local(whole[m], (w0g, w0u, w0d)[m], s_w0.at[m]) for m in range(3)]
    w0_out[0].start()

    def store_gate(i):
        return local(gate_v.at[span(i, T)], gate_hbm.at[span(i, T)], s_gate.at[i])

    def store_at(i):
        return local(at_s.at[odd(i)], at_hbm.at[:, span(i, T)], s_at.at[odd(i)])

    def store_hidt(i):
        return local(hidt_s.at[odd(i)], hidt_hbm.at[:, span(i, T)], s_hidt.at[odd(i)])

    def store_up(i):
        return local(up_s.at[odd(i)], up_hbm.at[span(i, T // 2)], s_up.at[odd(i)])

    def store_h1(i):
        return local(h1_s.at[odd(i)], h1_hbm.at[span(i, T)], s_h1.at[odd(i)])

    turns = [[] for _ in range(TILES)]
    for n, p in enumerate(every(1)):
        turns[2 + n].append((at_beside, *p))
    for n, p in enumerate(every(2)):
        turns[5 + 2 * n].append((at_first, *p))

    @pl.loop(0, TILES)
    def _(i):
        in_turn(i, turns)

        @pl.when(i >= 2)
        def _():
            store_at(i - 2).wait()

        ks = pl.ds(pl.multiple_of((1 - x) * B, B), D - B)
        for rs in halves(i):
            for n in range(NF):
                gate_v[rs, columns(n)] += dot(a_v[rs, ks], wg_v[ks, columns(n)])
        at_s[odd(i)] = a_v[span(i, T)].T
        store_gate(i).start()
        store_at(i).start()

    at_end(1)
    own(1).wait_recv()
    w0_out[1].start()
    load_h(0).start()

    def up_tile(i):
        for half, rs in enumerate(halves(i)):
            j = 2 * i + half

            @pl.when(j >= 2)
            def _():
                store_up(j - 2).wait()

            a = a_v[rs]
            for n in range(NF):
                cs = columns(n)
                g = gate_v[rs, cs]
                u = dot(a, wu_v[:, cs])
                up_s[half, :, cs] = u
                hid_s[lax.rem(i, LAG_DOWN + 1), half * (T // 2):(half + 1) * (T // 2), cs] = (g * sigmoid(g) * u).astype(BF)
            store_up(j).start()

    def down_tile(i):
        k = odd(i)
        for half in range(2):
            rs = slice(half * (T // 2), (half + 1) * (T // 2))
            h1_s[k, rs] = hin[k, rs] + dot(hid_s[lax.rem(i, LAG_DOWN + 1), rs], wd_v[...]).astype(BF)
        hidt_s[k] = hid_s[lax.rem(i, LAG_DOWN + 1)].T
        store_h1(i).start()
        store_hidt(i).start()

    turns = [[] for _ in range(TILES)]
    for n, p in enumerate(every(2)):
        turns[LAG_DOWN - 1].append((at_beside, *p))
    for n, m in enumerate((3, 4, 5)):
        turns[1 + 2 * n] += [(at_first, *p) for p in every(m)]
        turns[3 + 2 * n] += [(at_beside, *p) for p in every(m)]

    @pl.loop(0, LAG_DOWN)
    def _(i):
        in_turn(i, turns[:LAG_DOWN])
        up_tile(i)

    at_end(2)
    own(2).wait_recv()
    w0_out[2].start()

    @pl.loop(LAG_DOWN, TILES + LAG_DOWN)
    def _(i):
        j = i - LAG_DOWN
        in_turn(j, turns[LAG_DOWN:])
        next_h(j)

        @pl.when(j >= 2)
        def _():
            store_h1(j - 2).wait()
            store_hidt(j - 2).wait()

        @pl.when(i < TILES)
        def _():
            up_tile(i)

        down_tile(j)

    for m in (3, 4, 5):
        at_end(m)
        own(m).wait_recv()
    for i in (TILES - 2, TILES - 1):
        done((store_h1(i), store_hidt(i), store_at(i), store_up(TILES + i)))
    for i in range(TILES):
        store_gate(i).wait()
    done(w0_out + saves)
    for m in range(6):
        own(m).wait_send()
        for f in (first, relay, pass_first, pass_beside):
            all_of(lambda *p: f(*p).wait_send(), m)


LAG_DOWN = 2


def forward(x, wg, wu, wd):
    S = jax.ShapeDtypeStruct
    V = pltpu.VMEM
    wide, deep = (D, FF), (FF, D)
    weights = [S(wide, BF), S(wide, BF), S(deep, BF)]
    pieces = (2, 2 * sum(PARTS))
    return pl.pallas_call(
        forward_kernel,
        out_shape=[S((TOK, D), BF), S((TOK, FF), F32), S((TOK, FF), F32), S((D, TOK), BF), S((FF, TOK), BF)] + weights + weights,
        in_specs=[ANY] * 4,
        out_specs=[ANY] * 11,
        scratch_shapes=[
            V(wide, BF), V(wide, BF), V(deep, BF), V(wg.shape[1:], BF), V(wu.shape[1:], BF), V(wd.shape[1:], BF),
            V((TOK, D), BF), V((TOK, FF), F32), V((2, T, D), BF), V((2, T // 2, FF), F32), V((2, D, T), BF),
            V((LAG_DOWN + 1, T, FF), BF), V((2, FF, T), BF), V((2, T, D), BF),
            *[DMA(pieces)] * 4, DMA((2, 6)), DMA((2, 3)), *[DMA((2,))] * 4, DMA((TILES,)), DMA((3,)), DMA((2,)),
        ],
        compiler_params=pltpu.CompilerParams(collective_id=0, has_side_effects=True, vmem_limit_bytes=VMEM_LIMIT),
        cost_estimate=pl.CostEstimate(flops=6 * TOK * D * FF, bytes_accessed=130_000_000, transcendentals=TOK * FF),
        name="forward",
    )(x, wg, wu, wd)


def dot_tn(a, b):
    return lax.dot_general(a, b, (((0,), (0,)), ((), ())), preferred_element_type=F32)

MESH = pl.DeviceIdType.MESH
def place4():
    r, s = lax.axis_index("r"), lax.axis_index("s")
    return r, r // 4, lax.rem(r, 4), s, s // 2, lax.rem(s, 2)


def full(shape):
    return pl.BlockSpec(shape, lambda i: (0,) * len(shape), pipeline_mode=pl.Buffered(1))


def tile(t, n):
    return pl.BlockSpec((t, n), lambda i: (i, 0))


def norm_back(da, h, dy):
    h, da = h.astype(F32), da.astype(BF).astype(F32)
    scale = lax.rsqrt(jnp.mean(h * h, -1, keepdims=True) + 1e-6)
    along = jnp.sum(da * h, -1, keepdims=True) * (scale * scale * scale * (1.0 / D))
    return dy + (da * scale - h * along).astype(BF)


def last_kernel(h_ref, dy_ref, wg, wu, wd, dh_ref, dg_ref, du_ref, hidt_ref, at_ref, a_s, hid_s):
    n_rows = h_ref.shape[0]
    for lo in range(0, n_rows, 512):
        r = slice(lo, lo + 512)
        h = h_ref[r].astype(F32)
        a_s[r] = (h * lax.rsqrt(jnp.mean(h * h, -1, keepdims=True) + 1e-6)).astype(BF)
    for lo in range(0, n_rows, 512):
        r = slice(lo, lo + 512)
        for n in range(NF):
            cs = columns(n)
            g, u = dot(a_s[r], wg[:, cs]), dot(a_s[r], wu[:, cs])
            back = dot_nt(dy_ref[r], wd[cs]).astype(BF).astype(F32)
            s = sigmoid(g)
            silu = g * s
            hid_s[r, cs] = (silu * u).astype(BF)
            dg_ref[r, cs] = (back * u * (s + silu * (1 - s))).astype(BF)
            du_ref[r, cs] = (back * silu).astype(BF)
    for lo in range(0, n_rows, 256):
        r = slice(lo, lo + 256)
        dh_ref[r] = norm_back(dot_nt(dg_ref[r], wg[...]) + dot_nt(du_ref[r], wu[...]), h_ref[r], dy_ref[r])
    at_ref[...] = a_s[...].T
    hidt_ref[...] = hid_s[...].T


def last_layer(h, dy, wg, wu, wd, t=1024):
    S = jax.ShapeDtypeStruct
    return pl.pallas_call(
        last_kernel,
        grid=(TOK // t,),
        in_specs=[tile(t, D), tile(t, D), full((D, FF)), full((D, FF)), full((FF, D))],
        out_specs=[tile(t, D), tile(t, FF), tile(t, FF), pl.BlockSpec((FF, t), lambda i: (0, i)), pl.BlockSpec((D, t), lambda i: (0, i))],
        out_shape=[S((TOK, D), BF), S((TOK, FF), BF), S((TOK, FF), BF), S((FF, TOK), BF), S((D, TOK), BF)],
        scratch_shapes=[pltpu.VMEM((t, D), BF), pltpu.VMEM((t, FF), BF)],
        compiler_params=pltpu.CompilerParams(vmem_limit_bytes=66_000_000),
        cost_estimate=pl.CostEstimate(flops=12 * TOK * D * FF, bytes_accessed=80_000_000, transcendentals=TOK * FF),
        name="last_layer",
    )(h, dy, wg, wu, wd)


OUT = (jax.ShapeDtypeStruct((2, 192, FF), BF),) * 2 + (jax.ShapeDtypeStruct((2, 448, D), BF),)
UNITS = 42
LAG = (0, 2, 5, 7, 10, 13, 15, 16)
HT = TOK // 16
SLOTS, QUARTER, HALF = 8, 64, D // 2
ND = 14


def gradient_kernel(dy_hbm, dh_hbm, x_hbm, at1, hidt1, dg1, du1, at0, hidt0, gate0, up0, w0g, w0u, w0d,
                    gg, gu, gd, dg0, du0, dx_hbm,
                    at_v, dy_v, hbuf, cbuf, gate_v, up_v, dht_v, dgo, duo, wd_v, wg_v, wu_v, xt_v, dxo, term,
                    snd0, rcv0, keep1, snd1, rcv1, keep2, snd2, rcv2, keep3, snd3, rcv3, fin,
                    s_at, s_dy, s_h, s_c, s_g, s_u, s_dh, s_dgo, s_duo, s_w, s_x, s_dx,
                    s0, s1, s2, s3, s4, s5, s_out):
    r, y, z, s, x, c = place4()
    partner = {"s": 2 * x + (1 - c)}
    across = {"s": 2 * (1 - x) + c}
    ypeer = {"r": lax.rem(r + 4, 8)}
    zs = [lax.rem(z + d, 4) for d in (1, 2, 3)]
    zpeers = [{"r": 4 * y + zz} for zz in zs]

    def remote(src, dst, sems, to):
        return pltpu.make_async_remote_copy(src_ref=src, dst_ref=dst, send_sem=sems[0], recv_sem=sems[1], device_id=to, device_id_type=MESH)

    def pair(sems, *at):
        return sems.at[(0, *at)], sems.at[(1, *at)]

    def to_partner(v):
        k = lax.rem(v, 4)
        return remote(snd0.at[k], rcv0.at[k], pair(s0, k), partner)

    def to_across(v):
        k = lax.rem(v, SLOTS)
        return remote(snd1.at[k], rcv1.at[k], pair(s1, k), across)

    def to_y(v):
        k = lax.rem(v, SLOTS)
        return remote(snd2.at[k], rcv2.at[k], pair(s2, k), ypeer)

    def to_z(v):
        k = lax.rem(v, SLOTS)
        return [remote(snd3.at[k, span(zz, 16)], rcv3.at[k, d], pair(s3, k, d), to)
                for d, (zz, to) in enumerate(zip(zs, zpeers))]

    def back_z(v):
        k = lax.rem(v, 16)
        p = fin.at[k, y, span(z, 16)]
        return [remote(p, p, pair(s4, k, d), to) for d, to in enumerate(zpeers)]

    def back_y(v):
        k = lax.rem(v, 16)
        return remote(fin.at[k, y], fin.at[k, y], pair(s5, k), ypeer)

    def half(i):
        return span(i, HALF, 128)

    def stage1(v):
        to_partner(v).wait()
        k, k1 = lax.rem(v, 4), lax.rem(v, SLOTS)
        keep1[k1] = term[k, 2 * x + c] + rcv0[k, x].astype(F32)
        snd1[k1] = (term[k, 2 * (1 - x) + c] + rcv0[k, 1 - x].astype(F32)).astype(BF)
        to_across(v).start()

    def stage2(v):
        to_across(v).wait()
        k = lax.rem(v, SLOTS)
        keep2[k] = keep1[k, :, half(y)] + rcv1[k, :, half(y)].astype(F32)
        snd2[k] = (keep1[k, :, half(1 - y)] + rcv1[k, :, half(1 - y)].astype(F32)).astype(BF)
        to_y(v).start()

    def stage3(v):
        to_y(v).wait()
        k = lax.rem(v, SLOTS)
        mine = span(z, 16)
        keep3[k] = keep2[k, mine] + rcv2[k, mine].astype(F32)
        snd3[k] = (keep2[k] + rcv2[k].astype(F32)).astype(BF)
        for copy in to_z(v):
            copy.start()

    def stage4(v):
        for copy in to_z(v):
            copy.wait()
        k = lax.rem(v, SLOTS)
        total = keep3[k]
        for d in range(3):
            total = total + rcv3[k, d].astype(F32)
        fin[lax.rem(v, 16), y, span(z, 16)] = total.astype(BF)
        for copy in back_z(v):
            copy.start()

    def stage5(v):
        for copy in back_z(v):
            copy.wait()
        back_y(v).start()

    def outward(v):
        k, n, layer = lax.rem(v, 16), lax.rem(v, 21) // 3, 1 - v // 21
        kind = lax.rem(v, 3)
        to_down = [pltpu.make_async_copy(fin.at[k, h], gd.at[layer, span(n, QUARTER), h * 384:(h + 1) * 384], s_out.at[k, h])
                   for h in range(2)]
        plans = [(kind == 0, to_down)]
        for m, ref in ((1, gg), (2, gu)):
            todo = []
            for i, (h, lo, width, row, at) in enumerate(((0, 0, 256, 0, 0), (0, 256, 128, 64, 0), (1, 0, 128, 64, 128), (1, 128, 256, 128, 0))):
                dst = ref.at[layer, row:row + 64, pl.ds(pl.multiple_of(256 * n + at, 128), width)]
                todo.append(pltpu.make_async_copy(fin.at[k, h, :, lo:lo + width], dst, s_out.at[k, i]))
            plans.append((kind == m, todo))
        return plans

    def stage6(v):
        back_y(v).wait()
        for chosen, copies in outward(v):
            @pl.when(chosen)
            def _():
                for copy in copies:
                    copy.start()

    def stage7(v):
        for chosen, copies in outward(v):
            @pl.when(chosen)
            def _():
                for copy in copies:
                    copy.wait()

    stages = (stage1, stage2, stage3, stage4, stage5, stage6, stage7)

    def exchange(t):
        for n in range(7, 0, -1):
            v = t - LAG[n]

            @pl.when((v >= 0) & (v < UNITS))
            def _():
                stages[n - 1](v)

    def send_off(v):
        k = lax.rem(v, 4)
        for j in range(2):
            snd0[k, j] = term[k, 2 * j + 1 - c].astype(BF)
        to_partner(v).start()

    def rows(ref, i):
        return ref.at[span(i, HT)]

    def loads_back(i):
        k = odd(i)
        return [pltpu.make_async_copy(rows(gate0, i), gate_v.at[k], s_g.at[k]), pltpu.make_async_copy(rows(up0, i), up_v.at[k], s_u.at[k]),
                pltpu.make_async_copy(rows(dh_hbm, i), dht_v.at[k], s_dh.at[k])]

    def stores_back(i):
        k = odd(i)
        return [pltpu.make_async_copy(dgo.at[k], rows(dg0, i), s_dgo.at[k]), pltpu.make_async_copy(duo.at[k], rows(du0, i), s_duo.at[k])]

    def loads_input(i):
        k = odd(i)
        return [pltpu.make_async_copy(rows(dg0, i), dgo.at[k], s_g.at[k]), pltpu.make_async_copy(rows(du0, i), duo.at[k], s_u.at[k]),
                pltpu.make_async_copy(rows(dh_hbm, i), dht_v.at[k], s_dh.at[k]), pltpu.make_async_copy(rows(x_hbm, i), xt_v.at[k], s_x.at[k])]

    def store_input(i):
        k = odd(i)
        return pltpu.make_async_copy(dxo.at[k], rows(dx_hbm, i), s_dx.at[k])

    def load_rows(src, n):
        return [pltpu.make_async_copy(src.at[span(NF * q + n, QUARTER)], hbuf.at[QUARTER * q:QUARTER * (q + 1)], s_h.at[q])
                for q in range(4)]

    def load_columns(src, n, k):
        return pltpu.make_async_copy(src.at[:, span(n, B)], cbuf.at[k], s_c.at[k])

    def go(copies):
        for copy in copies:
            copy.start()

    def done(copies):
        for copy in copies:
            copy.wait()

    def ready_back(i):
        @pl.when(i + 1 < 16)
        def _():
            go(loads_back(i + 1))

        done(loads_back(i))

        @pl.when(i >= 2)
        def _():
            done(stores_back(i - 2))

    def back(i):
        k = odd(i)
        for n in range(7):
            cs = columns(n)
            by = dot_nt(dht_v[k], wd_v[cs]).astype(BF).astype(F32)
            g, u = gate_v[k, :, cs], up_v[k, :, cs]
            sg = sigmoid(g)
            silu = g * sg
            dgo[k, :, cs] = (by * u * (sg + silu * (1 - sg))).astype(BF)
            duo[k, :, cs] = (by * silu).astype(BF)

    def down_unit(v):
        slot = lax.rem(v, 4)
        for p in range(2):
            o = dot(hbuf[128 * p:128 * (p + 1)], dy_v[...])
            for q in range(2):
                term[slot, 2 * p + q] = o[64 * q:64 * (q + 1)]

    def column_unit(v, k):
        slot = lax.rem(v, 4)
        for p in range(2):
            o = dot(at_v[384 * p:384 * (p + 1)], cbuf[k])
            for q in range(2):
                for b in range(3):
                    lo = 192 * q + 64 * b
                    term[slot, 2 * p + q, :, 256 * b:256 * (b + 1)] = o[lo:lo + 64]

    barrier = pltpu.get_barrier_semaphore()
    for to in (partner, across, ypeer, *zpeers):
        pl.semaphore_signal(barrier, inc=1, device_id=to, device_id_type=MESH)
    go(loads_back(0))
    load_wd = pltpu.make_async_copy(w0d, wd_v, s_w.at[0])
    load_wg = pltpu.make_async_copy(w0g, wg_v, s_w.at[1])
    load_wu = pltpu.make_async_copy(w0u, wu_v, s_w.at[2])
    load_wd.start()
    load_dy = pltpu.make_async_copy(dy_hbm, dy_v, s_dy)
    load_dh = pltpu.make_async_copy(dh_hbm, dy_v, s_dy)
    load_at1 = pltpu.make_async_copy(at1, at_v, s_at)
    load_at0 = pltpu.make_async_copy(at0, at_v, s_at)
    ready_back(0)
    load_dy.start()
    go(load_rows(hidt1, 0))
    load_wd.wait()
    back(0)
    go(stores_back(0))
    ready_back(1)
    back(1)
    go(stores_back(1))
    load_at1.start()
    for k, src in enumerate((dg1, du1)):
        load_columns(src, 0, k).start()
    pl.semaphore_wait(barrier, 6)
    load_dy.wait()

    def rest(n, layer, sources, k):
        v = 21 * (1 - layer) + 3 * n + 1 + k
        exchange(v)
        load_columns(sources[k], n, k).wait()
        if layer:
            i = 2 * (n + 1) + k
            ready_back(i)
            column_unit(v, k)
            back(i)
            go(stores_back(i))
        else:
            column_unit(v, k)
        send_off(v)

        @pl.when(n < 6)
        def _():
            load_columns(sources[k], n + 1, k).start()

    @pl.loop(0, 7)
    def _(n):
        exchange(3 * n)
        done(load_rows(hidt1, n))
        down_unit(3 * n)
        send_off(3 * n)

        @pl.when(n < 6)
        def _():
            go(load_rows(hidt1, n + 1))

        @pl.when(n == 0)
        def _():
            load_at1.wait()

        @pl.when(n == 6)
        def _():
            load_dh.start()
            go(load_rows(hidt0, 0))

        for k in range(2):
            rest(n, 1, (dg1, du1), k)

    done(stores_back(14))
    done(stores_back(15))
    load_at0.start()
    for k, src in enumerate((dg0, du0)):
        load_columns(src, 0, k).start()
    load_wg.start()
    load_wu.start()
    load_dh.wait()

    @pl.loop(0, 7)
    def _(n):
        exchange(21 + 3 * n)
        done(load_rows(hidt0, n))
        down_unit(21 + 3 * n)
        send_off(21 + 3 * n)

        @pl.when(n < 6)
        def _():
            go(load_rows(hidt0, n + 1))

        @pl.when(n == 0)
        def _():
            load_at0.wait()

        @pl.when(n == 6)
        def _():
            go(loads_input(0))

        for k in range(2):
            rest(n, 0, (dg0, du0), k)

    load_wg.wait()
    load_wu.wait()

    @pl.loop(0, ND)
    def _(i):
        k = odd(i)

        @pl.when(i + 1 < ND)
        def _():
            go(loads_input(i + 1))

        exchange(42 + i)
        done(loads_input(i))

        @pl.when(i >= 2)
        def _():
            store_input(i - 2).wait()

        dxo[k] = norm_back(dot_nt(dgo[k], wg_v[...]) + dot_nt(duo[k], wu_v[...]), xt_v[k], dht_v[k])
        store_input(i).start()

    for i in (ND - 2, ND - 1):
        store_input(i).wait()

    @pl.loop(UNITS + ND, UNITS + LAG[7])
    def _(t):
        exchange(t)


def gradients(dy, dh, x, at1, hidt1, dg1, du1, at0, hidt0, gate0, up0, w0g, w0u, w0d):
    S = jax.ShapeDtypeStruct
    V = pltpu.VMEM

    def two(n, dtype=BF):
        return V((2, HT, n), dtype)

    def slots(n, dtype=BF, rows=QUARTER, parts=None):
        if parts:
            return V((4 if rows == QUARTER else SLOTS, parts, rows, n), dtype)
        return V((SLOTS, rows, n), dtype)

    return pl.pallas_call(
        gradient_kernel,
        out_shape=OUT + (S((TOK, FF), BF), S((TOK, FF), BF), S((TOK, D), BF)),
        in_specs=[ANY] * 14,
        out_specs=(ANY,) * 6,
        scratch_shapes=[
            V((D, TOK), BF), V((TOK, D), BF), V((B, TOK), BF), V((2, TOK, B), BF), two(FF, F32), two(FF, F32),
            two(D), two(FF), two(FF), V((FF, D), BF), V((D, FF), BF), V((D, FF), BF),
            two(D), two(D), slots(D, F32, QUARTER, 4),
            slots(D, BF, QUARTER, 2), slots(D, BF, QUARTER, 2), slots(D, F32), slots(D), slots(D),
            slots(HALF, F32), slots(HALF), slots(HALF), slots(HALF, F32, QUARTER // 4), slots(HALF), slots(HALF, BF, QUARTER // 4, 3),
            V((2 * SLOTS, 2, QUARTER, HALF), BF),
            DMA, DMA, DMA((4,)), *[DMA((2,))] * 6, DMA((3,)), *[DMA((2,))] * 2,
            *[DMA((2, SLOTS))] * 3, DMA((2, SLOTS, 3)), DMA((2, 2 * SLOTS, 3)), DMA((2, 2 * SLOTS)), DMA((2 * SLOTS, 4)),
        ],
        compiler_params=pltpu.CompilerParams(collective_id=1, has_side_effects=True, vmem_limit_bytes=67_000_000),
        cost_estimate=pl.CostEstimate(flops=18 * TOK * D * FF, bytes_accessed=250_000_000, transcendentals=TOK * FF),
        name="gradients",
    )(dy, dh, x, at1, hidt1, dg1, du1, at0, hidt0, gate0, up0, w0g, w0u, w0d)


def finish_kernel(dx_in, gg, gu, gd, dg, du, wg, wu, h_ref, dh_ref, dx, ggo, guo, gdo, dx_v, gg_v, gu_v, gd_v, dxo, s_in, s_o, s_dx):
    i = pl.program_id(0)
    last = pl.num_programs(0) - 1
    head = pl.ds(0, ND * HT)
    takes = [pltpu.make_async_copy(a, b, s_in.at[n]) for n, (a, b) in enumerate(((dx_in.at[head], dx_v), (gg, gg_v), (gu, gu_v), (gd, gd_v)))]
    puts = [pltpu.make_async_copy(a, b, s_o.at[n]) for n, (a, b) in enumerate(((dx_v, dx.at[head]), (gg_v, ggo), (gu_v, guo), (gd_v, gdo)))]

    def store(j):
        return pltpu.make_async_copy(dxo.at[odd(j)], dx.at[span(ND + j, HT)], s_dx.at[odd(j)])

    @pl.when(i == 0)
    def _():
        for copy in takes:
            copy.start()

    @pl.when(i == last)
    def _():
        for copy in takes:
            copy.wait()
        for copy in puts:
            copy.start()

    @pl.when(i >= 2)
    def _():
        store(i - 2).wait()

    dxo[odd(i)] = norm_back(dot_nt(dg[...], wg[...]) + dot_nt(du[...], wu[...]), h_ref[...], dh_ref[...])
    store(i).start()

    @pl.when(i == last)
    def _():
        store(i - 1).wait()
        store(i).wait()
        for copy in puts:
            copy.wait()


def finish(dx_in, gg, gu, gd, dg, du, wg, wu, h, dh):
    S = jax.ShapeDtypeStruct
    V = pltpu.VMEM
    def at(n):
        return pl.BlockSpec((HT, n), lambda i: (i + ND, 0))
    return pl.pallas_call(
        finish_kernel,
        grid=(16 - ND,),
        in_specs=[ANY] * 4 + [at(FF), at(FF), full((D, FF)), full((D, FF)), at(D), at(D)],
        out_specs=(ANY,) * 4,
        out_shape=(S((TOK, D), BF),) + OUT,
        scratch_shapes=[V((ND * HT, D), BF), *[V(o.shape, BF) for o in OUT], V((2, HT, D), BF), DMA((4,)), DMA((4,)), DMA((2,))],
        compiler_params=pltpu.CompilerParams(vmem_limit_bytes=66_000_000),
        cost_estimate=pl.CostEstimate(flops=TOK * D * FF, bytes_accessed=40_000_000, transcendentals=0),
        name="finish",
    )(dx_in, gg, gu, gd, dg, du, wg, wu, h, dh)


def solution(mesh):
    def step(x, dy, wg, wu, wd):
        x, dy = x[0], dy[0]
        h1, gate, up, at0, hidt0, w0g, w0u, w0d, w1g, w1u, w1d = forward(x, wg, wu, wd)
        dh, dg1, du1, hidt1, at1 = last_layer(h1, dy, w1g, w1u, w1d)
        gg, gu, gd, dg0, du0, dx = gradients(dy, dh, x, at1, hidt1, dg1, du1, at0, hidt0, gate, up, w0g, w0u, w0d)
        dx, gg, gu, gd = finish(dx, gg, gu, gd, dg0, du0, w0g, w0u, x, dh)
        return dx[None], gg, gu, gd

    states, cut = P(("rep", "r", "s"), None, None), P(None, "s", None)
    return jax.shard_map(
        step,
        mesh=mesh,
        in_specs=(states, states) + (cut,) * 3,
        out_specs=(states,) + (P("rep", "s", None),) * 3,
        check_vma=False,
    )
```

time: 705 us -> 306 us (0.43)
  matrix products: 414 us -> 0 us
  Pallas kernels: 0 us -> 298 us
  waiting for transfers between devices: 205 us -> 0 us
  local copies, waits for them, and re-layouts: 34 us -> 0 us
  other arithmetic: 29.1 us -> 0 us
  between operations: 14.5 us -> 1.12 us
    dot_general x17 -> x0, matrix products: 414 us -> none  [the longest x6 149 us: layer(): up = jnp.dot(a, w['w_up'], preferred_element_type=jnp.float32)]
    pallas_call x0 -> x4, Pallas kernels: none -> 298 us  [the longest x1 148 us: gradients(): pl.pallas_call(gradient_kernel, out_shape=OUT + (S((TOK, FF), BF), S((TOK...]
    psum x1 -> x0, waiting for transfers between devices: 113 us -> none  [summed(): lax.psum(lax.psum_scatter(term, 's', scatter_dimension=0, tiled=True), 'r')]
    reduce_scatter x6 -> x0, waiting for transfers between devices: 61.8 us -> none  [summed(): lax.psum_scatter(term, 's', scatter_dimension=0, tiled=True)]
    all_gather x6 -> x0, waiting for transfers between devices: 28.4 us -> none  [fetched(): lax.all_gather(w[number], 's', axis=0, tiled=True)]
    unnamed x27 -> x0, local copies, waits for them, and re-layouts: 26.6 us -> none
    add_any x1 -> x0, other arithmetic: 9.5 us -> none  [normed(): wide = h.astype(jnp.float32)]
    broadcast_in_dim x1 -> x0, other arithmetic: 9.5 us -> none  [step(): by_h[None]]
  transfers between devices with their start and end apart: 13 -> 0, of which waited for: 8 -> 0; matrix products, arithmetic and copies ran while one was open for 51% -> 0% of each run, Pallas kernels for 0% -> 0%
where the time goes in v2:
time: 306 us; the launch traced here: 300 us
  Pallas kernels  298 us (97%)
    pallas_call x1, Pallas kernels, gradients(): pl.pallas_call(gradient_kernel, out_shape=OUT + (S((TOK, FF), BF), S((TOK...  148 us
    pallas_call x1, Pallas kernels, last_layer(): pl.pallas_call(last_kernel, grid=(TOK // t,), in_specs=[tile(t, D), tile(...  70.9 us
    pallas_call x1, Pallas kernels, forward(): pl.pallas_call(forward_kernel, out_shape=[S((TOK, D), BF), S((TOK, FF), F...  68.4 us
    pallas_call x1, Pallas kernels, finish(): pl.pallas_call(finish_kernel, grid=(16 - ND,), in_specs=[ANY] * 4 + [at(F...  11.5 us

profile of v2, /device:TPU:0, one launch (start us, length us, event | category | flops | bytes accessed | tf_op | source)
XLA Modules:
  0.0 299.6 jit_solution(14311255420364386196)
XLA Ops:
  0.6 68.4 %forward.1 = (bf16[4096,768]{1,0:T(8,128)(2,1)}, f32[4096,1792]{1,0:T(8,128)}, f32[4096,1792]{1,0:T(8,128)}, bf16[768,4096]{1,0:T(8,128)(2,1)}, bf16[1792,4096]{...) custom-call(bf16[4096,768]{1,0:T(8,128)(2,1)} %bitcast.3, ...), custom_call_target="tpu_custom_call" | custom-call | flops 33822867456 | bytes 130000000 | tf_op jit(solution)/shard_map/forward/pallas_call | solution.py:332
  69.1 70.9 %last_layer.1 = (bf16[4096,768]{1,0:T(8,128)(2,1)}, bf16[4096,1792]{1,0:T(8,128)(2,1)}, bf16[4096,1792]{1,0:T(8,128)(2,1)}, bf16[1792,4096]{1,0:T(8,128)(2,1)}, bf16[768,4096]{1,0:T(8,128)(2,1)}) custom-call(bf16[4096,768]{1,0:T(8,128)(2,1)} %get-tuple-element.30.h_ref, bf16[4096,768]{1,0:T(8,128)(2,1)} %bitcast.6, bf16[768,1792]{1,0:T(8,128)(2,1)} %get-tuple-element.31.wg, ...), custom_call_target="tpu_custom_call" | custom-call | flops 67645734912 | bytes 80000000 | tf_op jit(solution)/shard_map/last_layer/pallas_call | solution.py:399
  140.0 147.6 %gradients.1 = (bf16[2,192,1792]{2,1,0:T(8,128)(2,1)}, bf16[2,192,1792]{2,1,0:T(8,128)(2,1)}, bf16[2,448,768]{2,1,0:T(8,128)(2,1)}, bf16[4096,1792]{1,0:T(8,128)...) custom-call(bf16[4096,768]{1,0:T(8,128)(2,1)} %bitcast.7, ...), custom_call_target="tpu_custom_call" | custom-call | flops 101468602368 | bytes 250000000 | tf_op jit(solution)/shard_map/gradients/pallas_call | solution.py:766
  287.6 11.5 %finish.1 = (bf16[4096,768]{1,0:T(8,128)(2,1)}, bf16[2,192,1792]{2,1,0:T(8,128)(2,1)}, bf16[2,192,1792]{2,1,0:T(8,128)(2,1)}, bf16[2,448,768]{2,1,0:T(8,128)(2,1)}) custom-call(bf16[4096,768]{1,0:T(8,128)(2,1)} %get-tuple-element.46.dx_in, bf16[2,192,1792]{2,1,0:T(8,128)(2,1)} %get-tuple-element.47.gg, bf16[2,192,1792]{2,1,0:T(8,128)(2,1)} %get-tuple-element.48.gu, ...), custom_call_target="tpu_custom_call" | custom-call | flops 5637144576 | bytes 40000000 | tf_op jit(solution)/shard_map/finish/pallas_call | solution.py:829
